TPU v7x, 32 devices: a 4x4x1 block of a 4x4x8 slice. The times are simulated.
32 devices in a mesh: dp: 1 (over z), dcp: 32 (over y, x, core).
Axes of the slice: x: 4, y: 4, z: 1, core: 2. Of those that a mesh axis runs over, the one named last changes fastest.
The devices are a block of a 4x4x8 slice.
Arguments:
- q_abs: bfloat16 [64, 128, 576], P('dp', 'dcp')
- cache: bfloat16 [64, 16384, 576], P('dp', 'dcp')
- lengths: int32 [64], P('dp')
Outputs:
- output: bfloat16 [64, 128, 512], P('dp', 'dcp')
All inputs are finite; a program needn't handle non-finite values.
Results may differ from a plain program's by a relative error of at most 0.00794727.
Values are sent between devices in bfloat16 or wider.
A program may use at most 768 MiB of HBM per device.

v0:
```python
import jax
import jax.numpy as jnp
from jax import lax
from jax.sharding import PartitionSpec as P

ROPE = 64
SCALE = 192 ** -0.5


def partial_attention(q, blk, valid, lat):
    s = jnp.einsum('bhk,btk->bht', q, blk, preferred_element_type=jnp.float32) * SCALE
    s = jnp.where(valid[:, None, :], s, -jnp.inf)
    m = jnp.max(s, axis=2)
    m0 = jnp.where(jnp.isfinite(m), m, 0.0)
    p = jnp.exp(s - m0[:, :, None])
    l = jnp.sum(p, axis=2)
    pv = jnp.einsum('bht,btc->bhc', p.astype(jnp.bfloat16), blk[:, :, :lat], preferred_element_type=jnp.float32)
    has = l > 0.0
    l1 = jnp.where(has, l, 1.0)
    od = (pv / l1[:, :, None]).astype(jnp.bfloat16)
    lse = jnp.where(has, m0 + jnp.log(l1), -jnp.inf)
    return od, lse


def merge(od, lse, axis):
    mx = jnp.max(lse, axis=axis, keepdims=True)
    wt = jnp.exp(lse - mx)
    wt = wt / jnp.sum(wt, axis=axis, keepdims=True)
    return jnp.sum(wt[..., None] * od.astype(jnp.float32), axis=axis).astype(jnp.bfloat16)


def solution(mesh):
    n = mesh.shape['dcp']

    def local(q, cache, lengths):
        d = lax.axis_index('dcp')
        b, sl, wd = cache.shape
        lat = wd - ROPE
        qa = lax.all_gather(q, 'dcp', axis=1, tiled=True)
        pos = d * sl + jnp.arange(sl)
        valid = pos[None, :] < lengths[:, None]
        od, lse = partial_attention(qa, cache, valid, lat)
        h = od.shape[1]
        od = od.reshape(b, n, h // n, lat)
        lse = lse.reshape(b, n, h // n)
        od = lax.all_to_all(od, 'dcp', 1, 1, tiled=True)
        lse = lax.all_to_all(lse, 'dcp', 1, 1, tiled=True)
        return merge(od, lse, 1)

    return jax.shard_map(local, mesh=mesh, in_specs=(P('dp', 'dcp', None), P('dp', 'dcp', None), P('dp')), out_specs=P('dp', 'dcp', None), check_vma=False)
```

profile of v0, /device:TPU:103, one launch (start us, length us, event | category | flops | bytes accessed | tf_op | source)
XLA Modules:
  0.0 280.2 jit_solution(515786863100501199)
XLA Ops:
  6.5 0.0 all-gather.2.cloned.1.call-start
  6.6 1.7 copy.9
  8.3 0.1 all-gather.2.cloned.1.call-update
  8.3 0.7 broadcast_compare_fusion
  9.1 55.6 %all-gather.2.cloned.1.call-done = bf16[64,128,576]{2,0,1:T(8,128)(2,1)} async-done(((bf16[64,4,576]{2,0,1:T(8,128)(2,1)}), bf16[64,128,576]{2,0,1:T(8,128)(2,1)}) %all-gather.2.cloned.1.call-update) | async-done | bytes 9437200 | tf_op jit(solution)/shard_map/all_gather | solution.py:39
  64.7 25.4 %fusion.2 = (f32[64,128]{1,0:T(8,128)S(1)}, f32[64,128,512]{2,1,0:T(8,128)}) fusion(pred[64,512]{1,0:T(8,128)(4,1)S(1)} %broadcast_compare_fusion, bf16[64,512,576]{1,2,0:T(8,128)(2,1)} %param.4, bf16[64,128,576]{2,0,1:T(8,128)(2,1)} %all-gather.2.cloned.1.call-done), kind=kOutput, calls=%fused_computation.6 | convolution fusion | flops 4844412928 | bytes 64028672 | tf_op jit(solution)/shard_map/bhk,btk->bht/dot_general | solution.py:11
  90.1 0.1 copy.12
  90.2 8.3 %fusion.4 = f32[64,128]{1,0:T(8,128)S(1)} fusion(f32[64,128,512]{2,1,0:T(8,128)} %get-tuple-element.6, f32[64,128]{1,0:T(8,128)S(1)} %is-finite_select_fusion.1, pred[64,512]{1,0:T(8,128)(4,1)S(1)} %broadcast_compare_fusion), kind=kLoop, calls=%fused_computation.8 | loop fusion | flops 16769024 | bytes 16875520 | tf_op jit(solution)/shard_map/reduce_sum | solution.py:16
  98.5 0.1 copy.11
  98.7 0.7 reshape.45
  99.4 4.5 %all-to-all-start = ((f32[32,1,256]{2,1,0:T(1,128)}), f32[32,1,256]{2,1,0:T(1,128)S(1)}, u32[]{:S(2)}, u32[]{:S(2)}) async-start(f32[32,1,256]{2,1,0:T(1,128)} %reshape.45), calls=%async_computation | async-start | bytes 65536 | tf_op jit(solution)/shard_map/all_to_all | solution.py:47
  103.9 22.1 %divide_convert_fusion = bf16[64,128,512]{2,1,0:T(8,128)(2,1)} fusion(bf16[64,512,576]{1,2,0:T(8,128)(2,1)} %param.4, f32[64,128,512]{2,1,0:T(8,128)} %get-tuple-element.6, f32[64,128]{1,0:T(8,128)S(1)} %compare_select_fusion, f32[64,128]{1,0:T(8,128)S(1)} %is-finite_select_fusion.1, pred[64,512]{1,0:T(8,128)(4,1)S(1)} %broadcast_compare_fusion), kind=kOutput, calls=%fused_computation.3 | convolution fusion | flops 4320133120 | bytes 58818560 | tf_op jit(solution)/shard_map/bht,btc->bhc/dot_general | solution.py:17
  126.0 12.6 %reshape.44 = bf16[64,32,4,512]{3,2,1,0:T(4,128)(2,1)} reshape(bf16[64,128,512]{2,1,0:T(8,128)(2,1)} %divide_convert_fusion) | data formatting | bytes 16777216 | tf_op jit(solution)/shard_map/reshape | solution.py:44
  138.5 8.1 %copy.15 = bf16[64,32,4,512]{3,2,0,1:T(4,128)(2,1)} copy(bf16[64,32,4,512]{3,2,1,0:T(4,128)(2,1)} %reshape.44) | data formatting | bytes 16777216 | tf_op jit(solution)/shard_map/reshape | solution.py:44
  146.7 0.0 all-to-all-done
  146.7 6.3 %all-to-all-start.1 = ((bf16[64,32,4,512]{3,2,0,1:T(4,128)(2,1)}), bf16[64,32,4,512]{3,2,0,1:T(4,128)(2,1)}, u32[]{:S(2)}, u32[]{:S(2)}) async-start(bf16[64,32,4,512]{3,2,0,1:T(4,128)(2,1)} %copy.15), calls=%async_computation.1 | async-start | bytes 16777216 | tf_op jit(solution)/shard_map/all_to_all | solution.py:46
  153.0 0.5 broadcast.38
  153.5 0.7 reduce
  154.3 0.1 reshape.46
  154.4 0.1 fusion.19
  154.5 0.4 copy.13
  154.9 111.3 %all-to-all-done.1 = bf16[64,32,4,512]{3,2,0,1:T(4,128)(2,1)} async-done(((bf16[64,32,4,512]{3,2,0,1:T(4,128)(2,1)}), bf16[64,32,4,512]{3,2,0,1:T(4,128)(2,1)}, u32[]{:S(2)}, u32[]{:S(2)}) %all-to-all-start.1) | async-done | bytes 8388640 | tf_op jit(solution)/shard_map/all_to_all | solution.py:46
  266.2 7.2 %multiply_reduce_fusion = bf16[64,4,512]{2,1,0:T(4,128)(2,1)} fusion(bf16[64,32,4,512]{3,2,0,1:T(4,128)(2,1)} %all-to-all-done.1, f32[64,32,4]{2,0,1:T(8,128)S(1)} %copy.13), kind=kLoop, calls=%fused_computation.2 | loop fusion | flops 12451840 | bytes 8683520 | tf_op jit(solution)/shard_map/reduce_sum | solution.py:29
  (6 shorter events, 0.1 us)
Async XLA Ops:
  6.5 58.1 %all-gather.2.cloned.1.call-start = ((), (), s32[]{:S(2)}) async-start(), calls=%async_computation.2 | async-start | bytes 10813440 | tf_op jit(solution)/shard_map/all_gather | solution.py:39
  99.4 47.3 %all-to-all-start = ((f32[32,1,256]{2,1,0:T(1,128)}), f32[32,1,256]{2,1,0:T(1,128)S(1)}, u32[]{:S(2)}, u32[]{:S(2)}) async-start(f32[32,1,256]{2,1,0:T(1,128)} %reshape.45), calls=%async_computation | async-start | bytes 65536 | tf_op jit(solution)/shard_map/all_to_all | solution.py:47
  146.7 119.5 %all-to-all-start.1 = ((bf16[64,32,4,512]{3,2,0,1:T(4,128)(2,1)}), bf16[64,32,4,512]{3,2,0,1:T(4,128)(2,1)}, u32[]{:S(2)}, u32[]{:S(2)}) async-start(bf16[64,32,4,512]{3,2,0,1:T(4,128)(2,1)} %copy.15), calls=%async_computation.1 | async-start | bytes 16777216 | tf_op jit(solution)/shard_map/all_to_all | solution.py:46
Sparse Core Ops, SparseCore 0:
  9.4 55.2 all-gather.1
where the time goes:
time: 281 us; the launch traced here: 280 us
  waiting for transfers between devices  167 us (59%)
  matrix products  47.4 us (17%)
  local copies, waits for them, and re-layouts  24.3 us (9%)
  other arithmetic  17.2 us (6%)
  between operations  13.5 us (5%)
  starting transfers between devices  10.8 us (4%)
    all_to_all x1, waiting for transfers between devices, local(): od = lax.all_to_all(od, 'dcp', 1, 1, tiled=True)  111 us
    all_gather x1, waiting for transfers between devices, local(): qa = lax.all_gather(q, 'dcp', axis=1, tiled=True)  55.6 us
    dot_general x1, matrix products, partial_attention(): jnp.einsum('bhk,btk->bht', q, blk, preferred_element_type=jnp.float32)  25.4 us
    dot_general x1, matrix products, partial_attention(): jnp.einsum('bht,btc->bhc', p.astype(jnp.bfloat16), blk[:, :, :lat], prefe...  22.1 us
    reshape x2, local copies, waits for them, and re-layouts, local(): od = od.reshape(b, n, h // n, lat)  20.7 us
    reduce_sum x1, other arithmetic, partial_attention(): l = jnp.sum(p, axis=2)  8.35 us
    reduce_sum x1, other arithmetic, merge(): jnp.sum(wt[..., None] * od.astype(jnp.float32), axis=axis)  7.18 us
    all_to_all x1, starting transfers between devices, local(): od = lax.all_to_all(od, 'dcp', 1, 1, tiled=True)  6.32 us
  transfers between devices with their start and end apart: 3, of which 2 were waited for; matrix products, arithmetic and copies ran while one was open for 16% of the time, Pallas kernels for 0%

commit v1 on v0

v1 whole, which is shorter than its diff:
```python
import functools

import jax
import jax.numpy as jnp
from jax import lax
from jax.experimental import pallas as pl
from jax.experimental.pallas import tpu as pltpu
from jax.sharding import PartitionSpec as P

ROPE = 64
SCALE = 192 ** -0.5
SIDE = 4
NS = 4
NB = 8
NEG = float('-inf')
F32 = jnp.float32
BF16 = jnp.bfloat16

LAG_P1F, LAG_P1R, LAG_FW, LAG_FR, LAG_C = 0, 1, 2, 3, 4
LAG_1, LAG_2, LAG_3, LAG_4, LAG_5 = 5, 6, 7, 8, 9


def softweights(parts):
    m = functools.reduce(jnp.maximum, parts)
    m0 = jnp.where(m == NEG, 0.0, m)
    ws = [jnp.exp(x - m0) for x in parts]
    tot = functools.reduce(jnp.add, ws)
    inv = 1.0 / jnp.where(tot == 0.0, 1.0, tot)
    return [w * inv for w in ws], m0 + jnp.log(tot)


def roll(x, shift):
    return pltpu.roll(x, shift % 128, 1)


def kernel(nc, len_ref, q_ref, cache_ref, out_ref,
           qraw, qm, qp, cbuf, cols, o_mine, o_send, o_recv, lse_own, lse_recv, lse_c, lse_r,
           fd_s, fd_r, m_s, m_r, acc, fd2_s, fd2_r, m2_s, m2_r, acc2,
           csem, s_p1, r_p1, s_p2, r_p2, s_qp, r_qp, s_o, r_o, s_fd, r_fd, s_m, r_m, s_fd2, r_fd2, s_m2, r_m2):
    me = lax.axis_index('dcp')
    core = me % 2
    x = (me // 2) % SIDE
    y = me // (2 * SIDE)
    nseq = q_ref.shape[0]
    sl = cbuf.shape[1]
    lat = out_ref.shape[2]
    lt = lat // 128
    half = NS // 2
    nt = qm.shape[2]
    ht = nt // 2

    def dev(xx, yy, cc):
        return {'dcp': (((yy + SIDE) % SIDE) * SIDE + (xx + SIDE) % SIDE) * 2 + cc}

    def small(ci, step):
        c = ci % 2
        return dev(x + (1 - c) * step, y + c * step, core)

    def big(ci, step):
        c = ci % 2
        return dev(x + c * step, y + (1 - c) * step, core)

    partner = dev(x, y, 1 - core)

    def first(ci):
        return (ci % 2) * (nseq // 2) + (ci // 2) * NS

    def rcopy(src, dst, ssem, rsem, to):
        return pltpu.make_async_remote_copy(src_ref=src, dst_ref=dst, send_sem=ssem, recv_sem=rsem, device_id=to,
                                            device_id_type=pl.DeviceIdType.MESH)

    def fetch(t):
        ci, s = t // NS, t % NS
        b = first(ci) + s
        return pltpu.make_async_copy(cache_ref.at[b], cbuf.at[t % NB], csem.at[t % NB])

    for t in range(NB):
        fetch(t).start()

    barrier = pltpu.get_barrier_semaphore()
    for to in (dev(x + 1, y, core), dev(x - 1, y, core), dev(x, y + 1, core), dev(x, y - 1, core), partner):
        pl.semaphore_signal(barrier, inc=1, device_id=to, device_id_type=pl.DeviceIdType.MESH)
    pl.semaphore_wait(barrier, 5)

    def p1(ci, d):
        sq = pl.ds(first(ci), NS)
        return rcopy(q_ref.at[sq], qraw.at[d, sq], s_p1.at[d], r_p1.at[ci, d], small(ci, 1 - 2 * d))

    def p1f(ci, d):
        sq = pl.ds(first(ci) + d * half, half)
        return rcopy(qraw.at[d, sq], qraw.at[2, sq], s_p1.at[2 + d], r_p1.at[ci, 2 + d], small(ci, 1 - 2 * d))

    def p2(ci, d):
        return rcopy(qm.at[0, ci], qm.at[3 - 2 * d, ci], s_p2.at[d], r_p2.at[ci, d], big(ci, 1 - 2 * d))

    def p2f(ci, d):
        tl = pl.ds(d * ht, ht)
        return rcopy(qm.at[3 - 2 * d, ci, tl], qm.at[2, ci, tl], s_p2.at[2 + d], r_p2.at[ci, 2 + d], big(ci, 1 - 2 * d))

    def toq(ci, slot):
        return rcopy(qm.at[slot, ci], qp.at[slot, ci], s_qp.at[slot], r_qp.at[ci, slot], partner)

    def too(ci):
        return rcopy(o_send.at[ci], o_recv.at[ci], s_o.at[0], r_o.at[ci, 0], partner)

    def tol(ci):
        return rcopy(lse_own.at[ci], lse_recv.at[ci], s_o.at[1], r_o.at[ci, 1], partner)

    def fd(ci, d):
        return rcopy(fd_s.at[d, ci], fd_r.at[d, ci], s_fd.at[d], r_fd.at[ci, d], big(ci, 1 - 2 * d))

    def mm(ci, d):
        return rcopy(m_s.at[d, ci], m_r.at[d, ci], s_m.at[d], r_m.at[ci, d], big(ci, 1 - 2 * d))

    def fd2(ci, d):
        return rcopy(fd2_s.at[d, ci], fd2_r.at[d, ci], s_fd2.at[d], r_fd2.at[ci, d], small(ci, 1 - 2 * d))

    def mm2(ci, d):
        return rcopy(m2_s.at[d, ci], m2_r.at[d, ci], s_m2.at[d], r_m2.at[ci, d], small(ci, 1 - 2 * d))

    def st_p1f(ci):
        for d in range(2):
            p1(ci, d).wait_recv()
            p1f(ci, d).start()

    def st_p1r(ci):
        for d in range(2):
            p1f(ci, d).wait_recv()
        ropes = []
        for s in range(NS):
            b = first(ci) + s
            rows = [q_ref[b], qraw[1, b], qraw[2, b], qraw[0, b]]
            rows = jnp.concatenate([r.astype(F32) for r in rows], axis=0)
            for l in range(lt):
                qm[0, ci, s * lt + l] = rows[:, l * 128:(l + 1) * 128].astype(BF16)
            ropes.append(rows[:, lat:lat + ROPE])
            if s % 2:
                qm[0, ci, NS * lt + s // 2] = jnp.concatenate(ropes[s - 1:s + 1], axis=1).astype(BF16)
        for d in range(2):
            p2(ci, d).start()
        toq(ci, 0).start()

    def st_fw(ci):
        for d in range(2):
            p2(ci, d).wait_recv()
            p2f(ci, d).start()
        toq(ci, 3).start()
        toq(ci, 1).start()

    def st_fr(ci):
        for d in range(2):
            p2f(ci, d).wait_recv()
        toq(ci, 2).start()

    lane128 = lax.broadcasted_iota(jnp.int32, (128, 128), 1)

    def st_c(ci):
        for slot in range(SIDE):
            toq(ci, slot).wait_recv()

        def pair(k, _):
            for u in range(2):
                s = 2 * k + u
                t = ci * NS + s
                b = first(ci) + s
                fetch(t).wait()
                tiles = []
                for l in range(lt):
                    i = s * lt + l
                    tiles.append(jnp.concatenate([qm[:, ci, i].reshape(64, 128), qp[:, ci, i].reshape(64, 128)], axis=0))
                i = NS * lt + k
                r = jnp.concatenate([qm[:, ci, i].reshape(64, 128), qp[:, ci, i].reshape(64, 128)], axis=0)
                tiles.append(r[:, u * ROPE:(u + 1) * ROPE])
                q = jnp.concatenate(tiles, axis=1)
                blk = cbuf.at[t % NB]
                sc = lax.dot_general(q, blk[...], (((1,), (1,)), ((), ())), preferred_element_type=F32) * SCALE
                pos = me * sl + lax.broadcasted_iota(jnp.int32, sc.shape, 1)
                sc = jnp.where(pos < len_ref[b], sc, NEG)
                m = jnp.max(sc, axis=1, keepdims=True)
                m0 = jnp.where(m == NEG, 0.0, m)
                p = jnp.exp(sc - m0)
                ls = jnp.sum(p, axis=1, keepdims=True)
                pv = lax.dot_general(p.astype(BF16), blk[:, :lat], (((1,), (0,)), ((), ())), preferred_element_type=F32)
                l1 = jnp.where(ls > 0.0, ls, 1.0)
                o = (pv * (1.0 / l1)).astype(BF16)
                lse = m0 + jnp.log(ls)
                cols[...] = jnp.where(lane128 == s, lse, cols[...])
                for slot in range(2 * SIDE):
                    to = o_mine if slot < SIDE else o_send
                    for l in range(lt):
                        to[ci, (s * SIDE + slot % SIDE) * lt + l] = o[slot * 16:(slot + 1) * 16, l * 128:(l + 1) * 128]

            for u in range(2):
                t = ci * NS + 2 * k + u + NB

                @pl.when(t < nc * NS)
                def _():
                    fetch(t).start()
            return 0

        lax.fori_loop(0, half, pair, 0)
        lse_own[ci] = cols[...].T[:8]
        too(ci).start()
        tol(ci).start()

    row8 = lax.broadcasted_iota(jnp.int32, (8, 128), 0)
    lane8 = lax.broadcasted_iota(jnp.int32, (8, 128), 1)

    def st_1(ci):
        too(ci).wait_recv()
        tol(ci).wait_recv()
        own = lse_own[ci]
        (wa, wb), lse = softweights([own, roll(lse_recv[ci], 64)])
        lse_c[ci] = lse
        wt = jnp.where(lane8 < 64, wa, roll(wb, 64)).T
        for d in range(2):
            fd_s[d, ci, NS * 2 * lt] = lse
        u = 2 * lt
        for s in range(NS):
            hf, sh = s // half, s % half
            for slot in range(SIDE):
                i = pl.ds((s * SIDE + slot) * lt, lt)
                ca = wt[slot * 16:(slot + 1) * 16, s:s + 1][None]
                cb = wt[64 + slot * 16:64 + (slot + 1) * 16, s:s + 1][None]
                v = (ca * o_mine[ci, i].astype(F32) + cb * o_recv[ci, i].astype(F32)).reshape(u, 8, 128)
                if slot == 0:
                    acc[ci, s * u:(s + 1) * u] = v
                elif slot == 2:
                    fd_s[hf, ci, sh * u:(sh + 1) * u] = v
                else:
                    d = 0 if slot == 1 else 1
                    if hf == 1 - d:
                        fd_s[d, ci, (half + sh) * u:(half + sh + 1) * u] = v
                    else:
                        m_s[d, ci, sh * u:(sh + 1) * u] = v
        for d in range(2):
            fd(ci, d).start()

    def st_2(ci):
        for d in range(2):
            fd(ci, d).wait_recv()
        u = 2 * lt
        left, right = fd_r[0, ci, NS * u], fd_r[1, ci, NS * u]
        far = jnp.where(lane8 < 32, roll(left, -16), roll(right, 16))
        (wa, wb), lse = softweights([lse_c[ci], far])
        wt = jnp.where(lane8 < 64, wa, roll(wb, 64)).T
        for d in range(2):
            m_s[d, ci, half * u] = lse
            for sh in range(half):
                s = d * half + sh
                r = 16 if d == 0 else 48
                ca = wt[r:r + 16, s:s + 1].reshape(1, 2, 8, 1)
                cb = wt[64 + r:80 + r, s:s + 1].reshape(1, 2, 8, 1)
                i = slice(sh * u, (sh + 1) * u)
                a = m_s[d, ci, i].reshape(lt, 2, 8, 128)
                f = fd_r[d, ci, i].reshape(lt, 2, 8, 128)
                m_s[d, ci, i] = (ca * a + cb * f).reshape(u, 8, 128)
            mm(ci, d).start()

    def st_3(ci):
        for d in range(2):
            mm(ci, d).wait_recv()
        u = 2 * lt
        left = roll(jnp.where(row8 < half, m_r[0, ci, half * u], fd_r[0, ci, NS * u]), -16)
        right = roll(jnp.where(row8 < half, fd_r[1, ci, NS * u], m_r[1, ci, half * u]), -48)
        (wo, wl, wr), lse = softweights([lse_c[ci], left, right])
        lse_r[ci] = lse
        for d in range(2):
            fd2_s[d, ci, NS * lt // 2] = lse
        wt = jnp.where(lane8 < 16, wo, jnp.where(lane8 < 32, roll(wl, 16), roll(wr, 32))).T
        res = []
        for s in range(NS):
            hf, sh = s // half, s % half
            im = slice(sh * u, (sh + 1) * u)
            idd = slice((half + sh) * u, (half + sh + 1) * u)
            lv = m_r[0, ci, im] if hf == 0 else fd_r[0, ci, idd]
            rv = fd_r[1, ci, idd] if hf == 0 else m_r[1, ci, im]
            vals = [acc[ci, s * u:(s + 1) * u], lv, rv]
            tot = 0.0
            for n, v in enumerate(vals):
                tot = tot + wt[n * 16:(n + 1) * 16, s:s + 1].reshape(1, 2, 8, 1) * v.reshape(lt, 2, 8, 128)
            res.append(tot.reshape(lt, 16, 128))
        for k in range(half):
            hf, kh = (2 * k) // half, k % (half // 2)
            for slot in range(SIDE):
                v = jnp.concatenate([res[2 * k][:, 4 * slot:4 * slot + 4], res[2 * k + 1][:, 4 * slot:4 * slot + 4]], axis=1)
                i = slice(kh * lt, (kh + 1) * lt)
                idd = slice((half // 2 + kh) * lt, (half // 2 + kh + 1) * lt)
                if slot == 0:
                    acc2[ci, k * lt:(k + 1) * lt] = v
                elif slot == 2:
                    fd2_s[hf, ci, i] = v
                else:
                    d = 0 if slot == 1 else 1
                    if hf == 1 - d:
                        fd2_s[d, ci, idd] = v
                    else:
                        m2_s[d, ci, i] = v
        for d in range(2):
            fd2(ci, d).start()

    def col2(wt, r, s):
        return jnp.concatenate([wt[r:r + 4, s:s + 1], wt[r:r + 4, s + 1:s + 2]], axis=0)[None]

    def st_4(ci):
        for d in range(2):
            fd2(ci, d).wait_recv()
        e = NS * lt // 2
        left, right = fd2_r[0, ci, e], fd2_r[1, ci, e]
        far = jnp.where(lane8 < 8, roll(left, -4), roll(right, 4))
        (wa, wb), lse = softweights([lse_r[ci], far])
        wt = jnp.where(lane8 < 64, wa, roll(wb, 64)).T
        for d in range(2):
            m2_s[d, ci, e // 2] = lse
            for kh in range(half // 2):
                s = d * half + 2 * kh
                r = 4 if d == 0 else 12
                i = slice(kh * lt, (kh + 1) * lt)
                m2_s[d, ci, i] = col2(wt, r, s) * m2_s[d, ci, i] + col2(wt, 64 + r, s) * fd2_r[d, ci, i]
            mm2(ci, d).start()

    def st_5(ci):
        for d in range(2):
            mm2(ci, d).wait_recv()
        e = NS * lt // 2
        left = roll(jnp.where(row8 < half, m2_r[0, ci, e // 2], fd2_r[0, ci, e]), -4)
        right = roll(jnp.where(row8 < half, fd2_r[1, ci, e], m2_r[1, ci, e // 2]), -12)
        (wo, wl, wr), _ = softweights([lse_r[ci], left, right])
        wt = jnp.where(lane8 < 16, wo, jnp.where(lane8 < 32, roll(wl, 16), roll(wr, 32))).T
        for k in range(half):
            hf, kh = (2 * k) // half, k % (half // 2)
            i = slice(kh * lt, (kh + 1) * lt)
            idd = slice((half // 2 + kh) * lt, (half // 2 + kh + 1) * lt)
            lv = m2_r[0, ci, i] if hf == 0 else fd2_r[0, ci, idd]
            rv = fd2_r[1, ci, idd] if hf == 0 else m2_r[1, ci, i]
            s = 2 * k
            tot = col2(wt, 0, s) * acc2[ci, k * lt:(k + 1) * lt] + col2(wt, 16, s) * lv + col2(wt, 32, s) * rv
            b = first(ci) + s
            for n in range(2):
                for l in range(lt):
                    out_ref[b + n, :, l * 128:(l + 1) * 128] = tot[l, 4 * n:4 * n + 4].astype(BF16)

    def send_p1(ci, _):
        for d in range(2):
            p1(ci, d).start()
        return 0

    cols[...] = jnp.zeros_like(cols)
    lax.fori_loop(0, nc, send_p1, 0)

    stages = [(LAG_P1F, st_p1f), (LAG_P1R, st_p1r), (LAG_FW, st_fw), (LAG_FR, st_fr), (LAG_C, st_c),
              (LAG_1, st_1), (LAG_2, st_2), (LAG_3, st_3), (LAG_4, st_4), (LAG_5, st_5)]

    def step(i, _):
        for lag, fn in stages:
            ci = i - lag

            @pl.when(jnp.logical_and(ci >= 0, ci < nc))
            def _():
                fn(ci)
        return 0

    lax.fori_loop(0, nc + LAG_5, step, 0)

    def drain(ref, sem):
        pltpu.make_async_copy(ref, ref, sem).wait()

    for d in range(2):
        drain(qraw.at[d], s_p1.at[d])
        drain(qraw.at[d, pl.ds(0, nseq // 2)], s_p1.at[2 + d])
        drain(qm.at[0], s_p2.at[d])
        drain(qm.at[0, :, pl.ds(0, ht)], s_p2.at[2 + d])
        drain(fd_s.at[d], s_fd.at[d])
        drain(m_s.at[d], s_m.at[d])
        drain(fd2_s.at[d], s_fd2.at[d])
        drain(m2_s.at[d], s_m2.at[d])
    for slot in range(SIDE):
        drain(qm.at[slot], s_qp.at[slot])
    drain(o_send, s_o.at[0])
    drain(lse_own, s_o.at[1])


def solution(mesh):
    assert mesh.shape['dcp'] == 2 * SIDE * SIDE

    def local(q, cache, lengths):
        nseq, heads, wd = q.shape
        sl = cache.shape[1]
        lat = wd - ROPE
        lt = lat // 128
        nc = nseq // NS
        nt = NS * lt + NS // 2
        vm = pltpu.VMEM
        dma = pltpu.SemaphoreType.DMA
        scratch = [
            vm((3, nseq, heads, wd), BF16),
            vm((SIDE, nc, nt, 16, 128), BF16),
            vm((SIDE, nc, nt, 16, 128), BF16),
            vm((NB, sl, wd), BF16),
            vm((128, 128), F32),
            vm((nc, NS * SIDE * lt, 16, 128), BF16),
            vm((nc, NS * SIDE * lt, 16, 128), BF16),
            vm((nc, NS * SIDE * lt, 16, 128), BF16),
            vm((nc, 8, 128), F32),
            vm((nc, 8, 128), F32),
            vm((nc, 8, 128), F32),
            vm((nc, 8, 128), F32),
            vm((2, nc, NS * 2 * lt + 1, 8, 128), F32),
            vm((2, nc, NS * 2 * lt + 1, 8, 128), F32),
            vm((2, nc, NS * lt + 1, 8, 128), F32),
            vm((2, nc, NS * lt + 1, 8, 128), F32),
            vm((nc, NS * 2 * lt, 8, 128), F32),
            vm((2, nc, NS * lt // 2 + 1, 8, 128), F32),
            vm((2, nc, NS * lt // 2 + 1, 8, 128), F32),
            vm((2, nc, NS * lt // 4 + 1, 8, 128), F32),
            vm((2, nc, NS * lt // 4 + 1, 8, 128), F32),
            vm((nc, NS * lt // 2, 8, 128), F32),
            dma((NB,)),
            dma((4,)), dma((nc, 4)),
            dma((4,)), dma((nc, 4)),
            dma((4,)), dma((nc, 4)),
            dma((2,)), dma((nc, 2)),
            dma((2,)), dma((nc, 2)),
            dma((2,)), dma((nc, 2)),
            dma((2,)), dma((nc, 2)),
            dma((2,)), dma((nc, 2)),
        ]
        return pl.pallas_call(
            functools.partial(kernel, nc),
            out_shape=jax.ShapeDtypeStruct((nseq, heads, lat), BF16),
            in_specs=[
                pl.BlockSpec(memory_space=pltpu.SMEM),
                pl.BlockSpec(memory_space=pltpu.VMEM),
                pl.BlockSpec(memory_space=pl.ANY),
            ],
            out_specs=pl.BlockSpec(memory_space=pltpu.VMEM),
            scratch_shapes=scratch,
            compiler_params=pltpu.CompilerParams(collective_id=0, has_side_effects=True, vmem_limit_bytes=67_000_000),
        )(lengths, q, cache)

    return jax.shard_map(local, mesh=mesh, in_specs=(P('dp', 'dcp', None), P('dp', 'dcp', None), P('dp')),
                         out_specs=P('dp', 'dcp', None), check_vma=False)
```

time: 281 us -> 178 us (0.63)
  the two profiles are of different devices: /device:TPU:103 before, /device:TPU:96 now
where the time goes in v1:
time: 178 us; the launch traced here: 176 us
  Pallas kernels  121 us (68%)
  local copies, waits for them, and re-layouts  55 us (31%)
    pallas_call x1, Pallas kernels, local(): pl.pallas_call(functools.partial(kernel, nc), out_shape=jax.ShapeDtypeStr...  121 us
    unnamed x2, local copies, waits for them, and re-layouts  55 us

profile of v1, /device:TPU:96, one launch (start us, length us, event | category | flops | bytes accessed | tf_op | source)
XLA Modules:
  0.0 176.2 jit_solution(2337436330486473327)
XLA Ops:
  0.0 53.2 %copy.4.cache_ref = bf16[64,512,576]{2,1,0:T(8,128)(2,1)} copy(bf16[64,512,576]{1,2,0:T(8,128)(2,1)} %param.4) | data formatting | bytes 75497472 | tf_op args[1]
  53.2 121.3 %shard_map.37 = bf16[64,4,512]{2,1,0:T(4,128)(2,1)} custom-call(s32[64]{0:T(128)} %len_ref.1, bf16[64,4,576]{2,1,0:T(4,128)(2,1)} %q_ref.1, bf16[64,512,576]{2,1,0:T(8,128)(2,1)} %copy.4.cache_ref), custom_call_target="tpu_custom_call" | custom-call | tf_op jit(solution)/shard_map/pallas_call | solution.py:428
  174.5 1.7 copy.6

commit v2 on v1

--- a/solution.py
+++ b/solution.py
@@ -42,7 +42,7 @@
     x = (me // 2) % SIDE
     y = me // (2 * SIDE)
     nseq = q_ref.shape[0]
-    sl = cbuf.shape[1]
+    sl = cbuf.shape[2]
     lat = out_ref.shape[2]
     lt = lat // 128
     half = NS // 2
@@ -173,14 +173,14 @@
                 tiles.append(r[:, u * ROPE:(u + 1) * ROPE])
                 q = jnp.concatenate(tiles, axis=1)
                 blk = cbuf.at[t % NB]
-                sc = lax.dot_general(q, blk[...], (((1,), (1,)), ((), ())), preferred_element_type=F32) * SCALE
+                sc = lax.dot_general(q, blk[...], (((1,), (0,)), ((), ())), preferred_element_type=F32) * SCALE
                 pos = me * sl + lax.broadcasted_iota(jnp.int32, sc.shape, 1)
                 sc = jnp.where(pos < len_ref[b], sc, NEG)
                 m = jnp.max(sc, axis=1, keepdims=True)
                 m0 = jnp.where(m == NEG, 0.0, m)
                 p = jnp.exp(sc - m0)
                 ls = jnp.sum(p, axis=1, keepdims=True)
-                pv = lax.dot_general(p.astype(BF16), blk[:, :lat], (((1,), (0,)), ((), ())), preferred_element_type=F32)
+                pv = lax.dot_general(p.astype(BF16), blk[:lat], (((1,), (1,)), ((), ())), preferred_element_type=F32)
                 l1 = jnp.where(ls > 0.0, ls, 1.0)
                 o = (pv * (1.0 / l1)).astype(BF16)
                 lse = m0 + jnp.log(ls)
@@ -396,7 +396,7 @@
             vm((3, nseq, heads, wd), BF16),
             vm((SIDE, nc, nt, 16, 128), BF16),
             vm((SIDE, nc, nt, 16, 128), BF16),
-            vm((NB, sl, wd), BF16),
+            vm((NB, wd, sl), BF16),
             vm((128, 128), F32),
             vm((nc, NS * SIDE * lt, 16, 128), BF16),
             vm((nc, NS * SIDE * lt, 16, 128), BF16),
@@ -436,7 +436,7 @@
             out_specs=pl.BlockSpec(memory_space=pltpu.VMEM),
             scratch_shapes=scratch,
             compiler_params=pltpu.CompilerParams(collective_id=0, has_side_effects=True, vmem_limit_bytes=67_000_000),
-        )(lengths, q, cache)
+        )(lengths, q, jnp.swapaxes(cache, 1, 2))
 
     return jax.shard_map(local, mesh=mesh, in_specs=(P('dp', 'dcp', None), P('dp', 'dcp', None), P('dp')),
                          out_specs=P('dp', 'dcp', None), check_vma=False)

time: 178 us -> 121 us (0.68); the launches traced: 176 us -> 121 us
  local copies, waits for them, and re-layouts: 55 us -> 1.74 us
    unnamed x2 -> x1, local copies, waits for them, and re-layouts: 55 us -> 1.74 us
where the time goes in v2:
time: 121 us
  Pallas kernels  120 us (99%)
  local copies, waits for them, and re-layouts  1.74 us (1%)
    pallas_call x1, Pallas kernels, local(): pl.pallas_call(functools.partial(kernel, nc), out_shape=jax.ShapeDtypeStr...  120 us

profile of v2, /device:TPU:96, one launch (start us, length us, event | category | flops | bytes accessed | tf_op | source)
XLA Modules:
  0.0 121.4 jit_solution(4536606038570794971)
XLA Ops:
  0.0 119.6 %shard_map.37 = bf16[64,4,512]{2,1,0:T(4,128)(2,1)} custom-call(s32[64]{0:T(128)} %len_ref.1, bf16[64,4,576]{2,1,0:T(4,128)(2,1)} %q_ref.1, bf16[64,576,512]{2,1,0:T(8,128)(2,1)} %bitcast.1), custom_call_target="tpu_custom_call" | custom-call | tf_op jit(solution)/shard_map/pallas_call | solution.py:428
  119.6 1.7 %copy.5 = bf16[64,4,512]{2,1,0:T(4,128)(2,1)} copy(bf16[64,4,512]{2,1,0:T(4,128)(2,1)} %shard_map.37) | data formatting | bytes 524288

commit v3 on v2

--- a/solution.py
+++ b/solution.py
@@ -13,11 +13,13 @@
 NS = 4
 NB = 8
 NEG = float('-inf')
+LOG2E = 1.4426950408889634
+LN2 = 0.6931471805599453
 F32 = jnp.float32
 BF16 = jnp.bfloat16
 
-LAG_P1F, LAG_P1R, LAG_FW, LAG_FR, LAG_C = 0, 1, 2, 3, 4
-LAG_1, LAG_2, LAG_3, LAG_4, LAG_5 = 5, 6, 7, 8, 9
+LAG_P1R, LAG_FW, LAG_FR, LAG_C = 0, 4, 8, 9
+LAG_1, LAG_2, LAG_3, LAG_4, LAG_5 = 10, 14, 18, 21, 24
 
 
 def softweights(parts):
@@ -158,47 +160,49 @@
         for slot in range(SIDE):
             toq(ci, slot).wait_recv()
 
-        def pair(k, _):
-            for u in range(2):
-                s = 2 * k + u
-                t = ci * NS + s
-                b = first(ci) + s
-                fetch(t).wait()
-                tiles = []
+        for s in range(NS):
+            fetch(ci * NS + s).wait()
+
+        def block(s):
+            return cbuf.at[(ci * NS + s) % NB]
+
+        def scores(s):
+            idx = [s * lt + l for l in range(lt)] + [NS * lt + s // 2]
+            tiles = [jnp.concatenate([qm[:, ci, i].reshape(64, 128), qp[:, ci, i].reshape(64, 128)], axis=0) for i in idx]
+            tiles[lt] = tiles[lt][:, s % 2 * ROPE:(s % 2 + 1) * ROPE]
+            q = jnp.concatenate(tiles, axis=1)
+            return lax.dot_general(q, block(s)[...], (((1,), (0,)), ((), ())), preferred_element_type=F32)
+
+        def attend(s, sc):
+            sc = jnp.where(pos < len_ref[first(ci) + s], sc * (SCALE * LOG2E), NEG)
+            m = jnp.max(sc, axis=1, keepdims=True)
+            m0 = jnp.where(m == NEG, 0.0, m)
+            p = jnp.exp2(sc - m0)
+            ls = jnp.sum(p, axis=1, keepdims=True)
+            pv = lax.dot_general(p.astype(BF16), block(s)[:lat], (((1,), (1,)), ((), ())), preferred_element_type=F32)
+            l1 = jnp.where(ls > 0.0, ls, 1.0)
+            o = (pv * (1.0 / l1)).astype(BF16)
+            for slot in range(2 * SIDE):
+                to = o_mine if slot < SIDE else o_send
                 for l in range(lt):
-                    i = s * lt + l
-                    tiles.append(jnp.concatenate([qm[:, ci, i].reshape(64, 128), qp[:, ci, i].reshape(64, 128)], axis=0))
-                i = NS * lt + k
-                r = jnp.concatenate([qm[:, ci, i].reshape(64, 128), qp[:, ci, i].reshape(64, 128)], axis=0)
-                tiles.append(r[:, u * ROPE:(u + 1) * ROPE])
-                q = jnp.concatenate(tiles, axis=1)
-                blk = cbuf.at[t % NB]
-                sc = lax.dot_general(q, blk[...], (((1,), (0,)), ((), ())), preferred_element_type=F32) * SCALE
-                pos = me * sl + lax.broadcasted_iota(jnp.int32, sc.shape, 1)
-                sc = jnp.where(pos < len_ref[b], sc, NEG)
-                m = jnp.max(sc, axis=1, keepdims=True)
-                m0 = jnp.where(m == NEG, 0.0, m)
-                p = jnp.exp(sc - m0)
-                ls = jnp.sum(p, axis=1, keepdims=True)
-                pv = lax.dot_general(p.astype(BF16), blk[:lat], (((1,), (1,)), ((), ())), preferred_element_type=F32)
-                l1 = jnp.where(ls > 0.0, ls, 1.0)
-                o = (pv * (1.0 / l1)).astype(BF16)
-                lse = m0 + jnp.log(ls)
-                cols[...] = jnp.where(lane128 == s, lse, cols[...])
-                for slot in range(2 * SIDE):
-                    to = o_mine if slot < SIDE else o_send
-                    for l in range(lt):
-                        to[ci, (s * SIDE + slot % SIDE) * lt + l] = o[slot * 16:(slot + 1) * 16, l * 128:(l + 1) * 128]
-
-            for u in range(2):
-                t = ci * NS + 2 * k + u + NB
-
-                @pl.when(t < nc * NS)
-                def _():
-                    fetch(t).start()
-            return 0
-
-        lax.fori_loop(0, half, pair, 0)
+                    to[ci, (s * SIDE + slot % SIDE) * lt + l] = o[slot * 16:(slot + 1) * 16, l * 128:(l + 1) * 128]
+            return m0 * LN2 + jnp.log(ls)
+
+        pos = me * sl + lax.broadcasted_iota(jnp.int32, (1, sl), 1)
+        sc = scores(0)
+        for s in range(NS):
+            after = scores(s + 1) if s + 1 < NS else None
+            lse = attend(s, sc)
+            cols[...] = jnp.where(lane128 == s, lse, cols[...])
+            sc = after
+
+        for s in range(NS):
+            t = (ci + NB // NS) * NS + s
+
+            @pl.when(t < nc * NS)
+            def _():
+                fetch(t).start()
+
         lse_own[ci] = cols[...].T[:8]
         too(ci).start()
         tol(ci).start()
@@ -346,9 +350,16 @@
         return 0
 
     cols[...] = jnp.zeros_like(cols)
+    def each(fn):
+        def body(ci, _):
+            fn(ci)
+            return 0
+        lax.fori_loop(0, nc, body, 0)
+
     lax.fori_loop(0, nc, send_p1, 0)
-
-    stages = [(LAG_P1F, st_p1f), (LAG_P1R, st_p1r), (LAG_FW, st_fw), (LAG_FR, st_fr), (LAG_C, st_c),
+    each(st_p1f)
+
+    stages = [(LAG_P1R, st_p1r), (LAG_FW, st_fw), (LAG_FR, st_fr), (LAG_C, st_c),
               (LAG_1, st_1), (LAG_2, st_2), (LAG_3, st_3), (LAG_4, st_4), (LAG_5, st_5)]
 
     def step(i, _):

time: 121 us -> 95.4 us (0.79)
  Pallas kernels: 120 us -> 93.5 us
    pallas_call x1, Pallas kernels: 120 us -> 93.5 us  [local(): pl.pallas_call(functools.partial(kernel, nc), out_shape=jax.ShapeDtypeStr...]
where the time goes in v3:
time: 95.4 us; the launch traced here: 95.3 us
  Pallas kernels  93.5 us (98%)
  local copies, waits for them, and re-layouts  1.74 us (2%)
    pallas_call x1, Pallas kernels, local(): pl.pallas_call(functools.partial(kernel, nc), out_shape=jax.ShapeDtypeStr...  93.5 us

profile of v3, /device:TPU:96, one launch (start us, length us, event | category | flops | bytes accessed | tf_op | source)
XLA Modules:
  0.0 95.3 jit_solution(12805508011274822520)
XLA Ops:
  0.0 93.5 %shard_map.37 = bf16[64,4,512]{2,1,0:T(4,128)(2,1)} custom-call(s32[64]{0:T(128)} %len_ref.1, bf16[64,4,576]{2,1,0:T(4,128)(2,1)} %q_ref.1, bf16[64,576,512]{2,1,0:T(8,128)(2,1)} %bitcast.1), custom_call_target="tpu_custom_call" | custom-call | tf_op jit(solution)/shard_map/pallas_call | solution.py:439
  93.5 1.7 %copy.5 = bf16[64,4,512]{2,1,0:T(4,128)(2,1)} copy(bf16[64,4,512]{2,1,0:T(4,128)(2,1)} %shard_map.37) | data formatting | bytes 524288

commit v4 on v3

--- a/solution.py
+++ b/solution.py
@@ -18,8 +18,8 @@
 F32 = jnp.float32
 BF16 = jnp.bfloat16
 
-LAG_P1R, LAG_FW, LAG_FR, LAG_C = 0, 4, 8, 9
-LAG_1, LAG_2, LAG_3, LAG_4, LAG_5 = 10, 14, 18, 21, 24
+LAG_P1R, LAG_FW, LAG_FR, LAG_C = 0, 5, 10, 11
+LAG_1, LAG_2, LAG_3, LAG_4, LAG_5 = 12, 16, 20, 24, 28
 
 
 def softweights(parts):

time: 95.4 us -> 93.2 us (0.977)
  Pallas kernels: 93.5 us -> 91.1 us
    pallas_call x1, Pallas kernels: 93.5 us -> 91.1 us  [local(): pl.pallas_call(functools.partial(kernel, nc), out_shape=jax.ShapeDtypeStr...]
where the time goes in v4:
time: 93.2 us; the launch traced here: 92.9 us
  Pallas kernels  91.1 us (98%)
  local copies, waits for them, and re-layouts  1.74 us (2%)
    pallas_call x1, Pallas kernels, local(): pl.pallas_call(functools.partial(kernel, nc), out_shape=jax.ShapeDtypeStr...  91.1 us

profile of v4, /device:TPU:96, one launch (start us, length us, event | category | flops | bytes accessed | tf_op | source)
XLA Modules:
  0.0 92.9 jit_solution(5803014461949457336)
XLA Ops:
  0.0 91.1 %shard_map.37 = bf16[64,4,512]{2,1,0:T(4,128)(2,1)} custom-call(s32[64]{0:T(128)} %len_ref.1, bf16[64,4,576]{2,1,0:T(4,128)(2,1)} %q_ref.1, bf16[64,576,512]{2,1,0:T(8,128)(2,1)} %bitcast.1), custom_call_target="tpu_custom_call" | custom-call | tf_op jit(solution)/shard_map/pallas_call | solution.py:439
  91.1 1.7 %copy.5 = bf16[64,4,512]{2,1,0:T(4,128)(2,1)} copy(bf16[64,4,512]{2,1,0:T(4,128)(2,1)} %shard_map.37) | data formatting | bytes 524288

commit v5 on v4

--- a/solution.py
+++ b/solution.py
@@ -35,8 +35,8 @@
     return pltpu.roll(x, shift % 128, 1)
 
 
-def kernel(nc, len_ref, q_ref, cache_ref, out_ref,
-           qraw, qm, qp, cbuf, cols, o_mine, o_send, o_recv, lse_own, lse_recv, lse_c, lse_r,
+def kernel(nc, len_ref, q_hbm, cache_ref, out_ref,
+           q_ref, qsem, qraw, qm, qp, cbuf, cols, o_mine, o_send, o_recv, lse_own, lse_recv, lse_c, lse_r,
            fd_s, fd_r, m_s, m_r, acc, fd2_s, fd2_r, m2_s, m2_r, acc2,
            csem, s_p1, r_p1, s_p2, r_p2, s_qp, r_qp, s_o, r_o, s_fd, r_fd, s_m, r_m, s_fd2, r_fd2, s_m2, r_m2):
     me = lax.axis_index('dcp')
@@ -76,12 +76,14 @@
         b = first(ci) + s
         return pltpu.make_async_copy(cache_ref.at[b], cbuf.at[t % NB], csem.at[t % NB])
 
-    for t in range(NB):
-        fetch(t).start()
-
     barrier = pltpu.get_barrier_semaphore()
     for to in (dev(x + 1, y, core), dev(x - 1, y, core), dev(x, y + 1, core), dev(x, y - 1, core), partner):
         pl.semaphore_signal(barrier, inc=1, device_id=to, device_id_type=pl.DeviceIdType.MESH)
+    own = pltpu.make_async_copy(q_hbm, q_ref, qsem)
+    own.start()
+    for t in range(NB):
+        fetch(t).start()
+    own.wait()
     pl.semaphore_wait(barrier, 5)
 
     def p1(ci, d):
@@ -404,6 +406,8 @@
         vm = pltpu.VMEM
         dma = pltpu.SemaphoreType.DMA
         scratch = [
+            vm((nseq, heads, wd), BF16),
+            dma(()),
             vm((3, nseq, heads, wd), BF16),
             vm((SIDE, nc, nt, 16, 128), BF16),
             vm((SIDE, nc, nt, 16, 128), BF16),
@@ -441,12 +445,12 @@
             out_shape=jax.ShapeDtypeStruct((nseq, heads, lat), BF16),
             in_specs=[
                 pl.BlockSpec(memory_space=pltpu.SMEM),
-                pl.BlockSpec(memory_space=pltpu.VMEM),
-                pl.BlockSpec(memory_space=pl.ANY),
+                pl.BlockSpec(memory_space=pltpu.HBM),
+                pl.BlockSpec(memory_space=pltpu.HBM),
             ],
             out_specs=pl.BlockSpec(memory_space=pltpu.VMEM),
             scratch_shapes=scratch,
-            compiler_params=pltpu.CompilerParams(collective_id=0, has_side_effects=True, vmem_limit_bytes=67_000_000),
+            compiler_params=pltpu.CompilerParams(collective_id=0, has_side_effects=True, vmem_limit_bytes=56_200_000),
         )(lengths, q, jnp.swapaxes(cache, 1, 2))
 
     return jax.shard_map(local, mesh=mesh, in_specs=(P('dp', 'dcp', None), P('dp', 'dcp', None), P('dp')),

time: 93.2 us -> 92.6 us (level)
  no operation moved by 1% of the time
where the time goes in v5:
time: 92.6 us; the launch traced here: 92.5 us
  Pallas kernels  91.2 us (98%)
  local copies, waits for them, and re-layouts  1.36 us (1%)
    pallas_call x1, Pallas kernels, local(): pl.pallas_call(functools.partial(kernel, nc), out_shape=jax.ShapeDtypeStr...  91.2 us

profile of v5, /device:TPU:96, one launch (start us, length us, event | category | flops | bytes accessed | tf_op | source)
XLA Modules:
  0.0 92.5 jit_solution(2848085678815236241)
XLA Ops:
  0.0 0.0 copy-start
  0.0 0.7 copy-done
  0.7 91.2 %shard_map.37 = bf16[64,4,512]{2,1,0:T(4,128)(2,1)S(1)} custom-call(s32[64]{0:T(128)S(1)} %copy-done, bf16[64,4,576]{2,1,0:T(4,128)(2,1)} %q_hbm.1, bf16[64,576,512]{2,1,0:T(8,128)(2,1)} %bitcast.1), custom_call_target="tpu_custom_call" | custom-call | tf_op jit(solution)/shard_map/pallas_call | solution.py:443
  91.8 0.7 copy.5
Async XLA Ops:
  0.0 0.7 copy-start
